TPU v7x, 32 devices: a whole 2x2x4 slice. The times are simulated.
32 devices in a mesh: span: 4 (over y, x), heads: 8 (over z, core).
Axes of the slice: x: 2, y: 2, z: 4, core: 2. Of those that a mesh axis runs over, the one named last changes fastest.
Arguments:
- latents: bfloat16 [4, 6144, 512], P(None, ('span', 'heads')), may hold values from -6 to 6
- rotary_rows: bfloat16 [4, 6144, 64], P(None, ('span', 'heads')), may hold values from -6 to 6
- latent_gain: float32 [512], replicated, may hold values from 0.25 to 1.75
- key_up: bfloat16 [512, 16, 128], P(None, 'heads'), may hold values from -0.25 to 0.25
- value_up: bfloat16 [512, 16, 128], P(None, 'heads'), may hold values from -0.25 to 0.25
Outputs:
- stored_keys: bfloat16 [4, 6144, 16, 192], P('span', None, 'heads')
- stored_values: bfloat16 [4, 6144, 16, 128], P('span', None, 'heads')
All inputs are finite; a program needn't handle non-finite values.
Results may differ from a plain program's by a relative error of at most 0.001.
Values may be sent and summed in bfloat16 or wider, within the bound.
A program may use at most 128 MiB of HBM per device.

v0:
```python
import jax
import jax.numpy as jnp
from jax import lax
from jax.sharding import PartitionSpec as P


def expand_rows(rows, rotary, key_up, value_up):
    wide_keys = jnp.einsum(
        "btr,rhk->bthk", rows, key_up, preferred_element_type=jnp.float32
    ).astype(jnp.bfloat16)
    shared = jnp.broadcast_to(rotary[:, :, None], wide_keys.shape[:3] + rotary.shape[2:])
    wide_values = jnp.einsum(
        "btr,rhk->bthk", rows, value_up, preferred_element_type=jnp.float32
    ).astype(jnp.bfloat16)
    return (jnp.concatenate([wide_keys, shared], axis=-1), wide_values)


def root_norm(vectors, row_gain):
    return (
        vectors * lax.rsqrt(jnp.mean(vectors * vectors, axis=-1, keepdims=True) + 1e-06) * row_gain
    )


def per_device(latents, rotary_rows, latent_gain, key_up, value_up):
    rows_ready = root_norm(latents.astype(jnp.float32), latent_gain).astype(jnp.bfloat16)
    rows_moved, rotary_moved = (
        lax.all_to_all(rows_ready, "span", split_axis=0, concat_axis=1, tiled=True),
        lax.all_to_all(rotary_rows, "span", split_axis=0, concat_axis=1, tiled=True),
    )
    rows_cut = rows_moved.reshape(
        rows_moved.shape[0], lax.axis_size("span"), -1, rows_moved.shape[2]
    )
    rotary_cut = rotary_moved.reshape(
        rotary_moved.shape[0], lax.axis_size("span"), -1, rotary_moved.shape[2]
    )
    rows_joined, rotary_joined = (
        lax.all_gather(rows_cut, "heads", axis=2, tiled=True),
        lax.all_gather(rotary_cut, "heads", axis=2, tiled=True),
    )
    rows_whole = rows_joined.reshape(rows_joined.shape[0], -1, rows_joined.shape[3])
    rotary_whole = rotary_joined.reshape(rotary_joined.shape[0], -1, rotary_joined.shape[3])
    stored_keys, stored_values = expand_rows(rows_whole, rotary_whole, key_up, value_up)
    return (stored_keys, stored_values)


def solution(mesh):
    in_specs = (
        P(None, ("span", "heads"), None),
        P(None, ("span", "heads"), None),
        P(),
        P(None, "heads", None),
        P(None, "heads", None),
    )
    out_specs = (P("span", None, "heads", None), P("span", None, "heads", None))
    return jax.shard_map(
        per_device, mesh=mesh, in_specs=in_specs, out_specs=out_specs, check_vma=False
    )
```

profile of v0, /device:TPU:0, one launch (start us, length us, event | category | flops | bytes accessed | tf_op | source)
XLA Modules:
  0.0 149.0 jit_solution(12033314378571793330)
XLA Ops:
  7.2 0.0 copy-start
  7.2 0.0 copy-start.2
  7.2 0.0 all-gather.4.cloned.1.call-start
  7.2 1.4 fusion.1
  8.7 1.4 fusion.3
  10.1 16.4 %all_to_all.8 = bf16[4,192,512]{2,1,0:T(8,128)(2,1)} all-to-all(bf16[4,192,512]{2,1,0:T(8,128)(2,1)S(1)} %fusion.3), channel_id=1, replica_groups=mesh['span'=4,'heads'=8] {'span'}, dimensions={0} | all-to-all | bytes 1572864 | tf_op jit(solution)/shard_map/all_to_all | solution.py:27
  26.5 0.0 all-gather.4.cloned.1.call-update
  26.5 3.3 %all-to-all-start.1 = ((bf16[4,192,64]{1,2,0:T(8,128)(2,1)}), bf16[4,192,64]{1,2,0:T(8,128)(2,1)S(1)}, u32[]{:S(2)}, u32[]{:S(2)}) async-start(bf16[4,192,64]{1,2,0:T(8,128)(2,1)} %param.6), calls=%async_computation.1 | async-start | bytes 262144 | tf_op jit(solution)/shard_map/all_to_all | solution.py:28
  29.9 0.0 copy-done.2
  29.9 0.2 copy.19
  30.1 4.8 %all-to-all-done.1 = bf16[4,192,64]{1,2,0:T(8,128)(2,1)S(1)} async-done(((bf16[4,192,64]{1,2,0:T(8,128)(2,1)}), bf16[4,192,64]{1,2,0:T(8,128)(2,1)S(1)}, u32[]{:S(2)}, u32[]{:S(2)}) %all-to-all-start.1) | async-done | bytes 98336 | tf_op jit(solution)/shard_map/all_to_all | solution.py:28
  34.9 0.2 copy.20
  35.0 31.3 %all-gather.1 = bf16[4,1536,64]{2,0,1:T(4,128)(2,1)S(1)} all-gather(bf16[4,192,64]{2,0,1:T(4,128)(2,1)S(1)} %copy.20), channel_id=3, replica_groups=mesh['span'=4,'heads'=8] {'heads'}, dimensions={1}, use_global_device_ids=true | all-gather | bytes 884736 | tf_op jit(solution)/shard_map/all_gather | solution.py:38
  66.4 1.2 copy.21
  67.5 0.1 copy.24
  67.7 35.9 %all-gather.4.cloned.1.call-done = bf16[4,1536,512]{2,1,0:T(8,128)(2,1)} async-done(((bf16[4,192,512]{2,1,0:T(8,128)(2,1)}), bf16[4,1536,512]{2,1,0:T(8,128)(2,1)}) %all-gather.4.cloned.1.call-update) | async-done | bytes 6291472 | tf_op jit(solution)/shard_map/all_gather | solution.py:37
  103.6 4.6 %fusion.5 = f32[6144,256]{0,1:S(1)} fusion(bf16[6144,512]{1,0:T(8,128)(2,1)} %bitcast.17, bf16[512,256]{0,1:T(8,128)(2,1)S(1)} %bitcast.21), kind=kOutput, calls=%fused_computation.11 | convolution fusion | flops 1610612736 | bytes 12845056
  108.2 0.0 copy-start.1
  108.2 0.4 convert_bitcast_fusion
  108.6 0.0 copy-done
  108.6 2.3 %copy-done.1 = bf16[4,1536,512]{2,1,0:T(8,128)(2,1)S(1)} copy-done((bf16[4,1536,512]{2,1,0:T(8,128)(2,1)S(1)}, bf16[4,1536,512]{2,1,0:T(8,128)(2,1)}, u32[]{:S(2)}) %copy-start.1) | copy-done | bytes 6291480
  111.0 1.8 %fusion = bf16[1,6144,2,128]{3,1,2,0:T(8,128)(2,1)S(1)} fusion(bf16[6144,512,1]{1,0,2:T(8,128)(2,1)S(1)} %bitcast.18, bf16[512,2,128]{2,1,0:T(2,128)(2,1)S(1)} %copy-done), kind=kOutput, calls=%fused_computation.1 | convolution fusion | flops 1612185600 | bytes 9699328 | tf_op jit(solution)/shard_map/btr,rhk->bthk/dot_general | solution.py:12
  112.8 26.8 %copy.23 = bf16[1,6144,2,128]{3,2,1,0:T(2,128)(2,1)} copy(bf16[1,6144,2,128]{3,1,2,0:T(8,128)(2,1)S(1)} %fusion) | data formatting | bytes 6291456
  139.5 0.1 broadcast_in_dim.10
  139.7 2.5 %pad_maximum_fusion = bf16[1,6144,2,192]{1,3,2,0:T(8,128)(2,1)} fusion(bf16[1,6144,2,64]{1,3,2,0:T(8,128)(2,1)S(1)} %broadcast_in_dim.10, bf16[1,6144,2,128]{1,3,2,0:T(8,128)(2,1)S(1)} %convert_bitcast_fusion), kind=kLoop, calls=%fused_computation.2 | loop fusion | flops 9437184 | bytes 9437184 | tf_op jit(solution)/shard_map/concatenate | solution.py:15
  (1 shorter events, 0.0 us)
Async XLA Ops:
  7.2 101.5 %copy-start = (bf16[512,2,128]{2,1,0:T(2,128)(2,1)S(1)}, bf16[512,2,128]{2,1,0:T(2,128)(2,1)}, u32[]{:S(2)}) copy-start(bf16[512,2,128]{2,1,0:T(2,128)(2,1)} %param.9) | copy-start | bytes 786436
  7.2 22.7 %copy-start.2 = (bf16[512,2,128]{2,1,0:T(2,128)(2,1)S(1)}, bf16[512,2,128]{2,1,0:T(2,128)(2,1)}, u32[]{:S(2)}) copy-start(bf16[512,2,128]{2,1,0:T(2,128)(2,1)} %param.8) | copy-start | bytes 786436
  7.2 96.4 %all-gather.4.cloned.1.call-start = ((), (), s32[]{:S(2)}) async-start(), calls=%async_computation.2 | async-start | bytes 7077888 | tf_op jit(solution)/shard_map/all_gather | solution.py:37
  26.5 8.3 %all-to-all-start.1 = ((bf16[4,192,64]{1,2,0:T(8,128)(2,1)}), bf16[4,192,64]{1,2,0:T(8,128)(2,1)S(1)}, u32[]{:S(2)}, u32[]{:S(2)}) async-start(bf16[4,192,64]{1,2,0:T(8,128)(2,1)} %param.6), calls=%async_computation.1 | async-start | bytes 262144 | tf_op jit(solution)/shard_map/all_to_all | solution.py:28
  108.2 2.8 %copy-start.1 = (bf16[4,1536,512]{2,1,0:T(8,128)(2,1)S(1)}, bf16[4,1536,512]{2,1,0:T(8,128)(2,1)}, u32[]{:S(2)}) copy-start(bf16[4,1536,512]{2,1,0:T(8,128)(2,1)} %all-gather.4.cloned.1.call-done) | copy-start | bytes 18874372
Sparse Core Ops, SparseCore 0:
  26.6 76.8 all-gather.3
where the time goes:
time: 149 us
  blocking collectives  47.8 us (32%)
  waiting for transfers between devices  40.7 us (27%)
  local copies, waits for them, and re-layouts  30.9 us (21%)
  between operations  14.2 us (10%)
  matrix products  6.4 us (4%)
  other arithmetic  5.74 us (4%)
  starting transfers between devices  3.38 us (2%)
    all_gather x1, waiting for transfers between devices, per_device(): lax.all_gather(rows_cut, 'heads', axis=2, tiled=True)  35.9 us
    all_gather x1, blocking collectives, per_device(): lax.all_gather(rotary_cut, 'heads', axis=2, tiled=True)  31.3 us
    unnamed x9, local copies, waits for them, and re-layouts  29.4 us
    all_to_all x1, blocking collectives, per_device(): lax.all_to_all(rows_ready, 'span', split_axis=0, concat_axis=1, tiled=True)  16.4 us
    all_to_all x1, waiting for transfers between devices, per_device(): lax.all_to_all(rotary_rows, 'span', split_axis=0, concat_axis=1, tiled=True)  4.81 us
    unnamed x1, matrix products  4.61 us
    all_to_all x1, starting transfers between devices, per_device(): lax.all_to_all(rotary_rows, 'span', split_axis=0, concat_axis=1, tiled=True)  3.34 us
  transfers between devices with their start and end apart: 2, of which 2 were waited for; matrix products, arithmetic and copies ran while one was open for 1% of the time, Pallas kernels for 0%

commit v1 on v0

--- a/solution.py
+++ b/solution.py
@@ -2,6 +2,18 @@
 import jax.numpy as jnp
 from jax import lax
 from jax.sharding import PartitionSpec as P
+
+
+def plan_slots(a0):
+    return jnp.concatenate(
+        lax.all_to_all(
+            jnp.stack(jnp.split(a0, lax.psum(1, axis_name="span"), axis=0)),
+            axis_name="span",
+            split_axis=0,
+            concat_axis=0,
+        ),
+        1,
+    )
 
 
 def expand_rows(rows, rotary, key_up, value_up):
@@ -24,7 +36,7 @@
 def per_device(latents, rotary_rows, latent_gain, key_up, value_up):
     rows_ready = root_norm(latents.astype(jnp.float32), latent_gain).astype(jnp.bfloat16)
     rows_moved, rotary_moved = (
-        lax.all_to_all(rows_ready, "span", split_axis=0, concat_axis=1, tiled=True),
+        plan_slots(rows_ready),
         lax.all_to_all(rotary_rows, "span", split_axis=0, concat_axis=1, tiled=True),
     )
     rows_cut = rows_moved.reshape(

time: 149 us -> 150 us (level)
  no operation moved by 1% of the time
where the time goes in v1:
time: 150 us; the launch traced here: 149 us
  blocking collectives  47.8 us (32%)
  waiting for transfers between devices  40.7 us (27%)
  local copies, waits for them, and re-layouts  31 us (21%)
  between operations  14.2 us (9%)
  matrix products  6.41 us (4%)
  other arithmetic  5.84 us (4%)
  starting transfers between devices  3.38 us (2%)
    all_gather x1, waiting for transfers between devices, per_device(): lax.all_gather(rows_cut, 'heads', axis=2, tiled=True)  35.9 us
    all_gather x1, blocking collectives, per_device(): lax.all_gather(rotary_cut, 'heads', axis=2, tiled=True)  31.3 us
    unnamed x9, local copies, waits for them, and re-layouts  29.4 us
    all_to_all x1, blocking collectives, plan_slots(): lax.all_to_all(jnp.stack(jnp.split(a0, lax.psum(1, axis_name='span'), axi...  16.4 us
    all_to_all x1, waiting for transfers between devices, per_device(): lax.all_to_all(rotary_rows, 'span', split_axis=0, concat_axis=1, tiled=True)  4.81 us
    unnamed x1, matrix products  4.61 us
    all_to_all x1, starting transfers between devices, per_device(): lax.all_to_all(rotary_rows, 'span', split_axis=0, concat_axis=1, tiled=True)  3.34 us
  transfers between devices with their start and end apart: 2, of which 2 were waited for; matrix products, arithmetic and copies ran while one was open for 1% of the time, Pallas kernels for 0%

profile of v1, /device:TPU:0, one launch (start us, length us, event | category | flops | bytes accessed | tf_op | source)
XLA Modules:
  0.0 149.2 jit_solution(4396283261866898691)
XLA Ops:
  7.2 0.0 copy-start
  7.2 0.0 copy-start.2
  7.2 0.0 all-gather.4.cloned.1.call-start
  7.2 1.4 fusion.1
  8.7 1.4 fusion.3
  10.1 0.1 slice_bitcast_fusion.3
  10.1 0.1 pad_maximum_fusion.1
  10.2 16.4 %all_to_all.14 = bf16[4,1,192,512]{3,2,1,0:T(8,128)(2,1)} all-to-all(bf16[4,1,192,512]{3,2,1,0:T(8,128)(2,1)S(1)} %pad_maximum_fusion.1), channel_id=1, replica_groups=mesh['span'=4,'heads'=8] {'span'}, dimensions={0} | all-to-all | bytes 1572864 | tf_op jit(solution)/shard_map/all_to_all | solution.py:9
  26.7 0.0 all-gather.4.cloned.1.call-update
  26.7 3.3 %all-to-all-start.1 = ((bf16[4,192,64]{1,2,0:T(8,128)(2,1)}), bf16[4,192,64]{1,2,0:T(8,128)(2,1)S(1)}, u32[]{:S(2)}, u32[]{:S(2)}) async-start(bf16[4,192,64]{1,2,0:T(8,128)(2,1)} %param.6), calls=%async_computation.1 | async-start | bytes 262144 | tf_op jit(solution)/shard_map/all_to_all | solution.py:40
  30.0 0.0 copy-done.2
  30.1 0.2 copy.19
  30.2 4.8 %all-to-all-done.1 = bf16[4,192,64]{1,2,0:T(8,128)(2,1)S(1)} async-done(((bf16[4,192,64]{1,2,0:T(8,128)(2,1)}), bf16[4,192,64]{1,2,0:T(8,128)(2,1)S(1)}, u32[]{:S(2)}, u32[]{:S(2)}) %all-to-all-start.1) | async-done | bytes 98336 | tf_op jit(solution)/shard_map/all_to_all | solution.py:40
  35.0 0.2 copy.20
  35.2 31.3 %all-gather.1 = bf16[4,1536,64]{2,0,1:T(4,128)(2,1)S(1)} all-gather(bf16[4,192,64]{2,0,1:T(4,128)(2,1)S(1)} %copy.20), channel_id=3, replica_groups=mesh['span'=4,'heads'=8] {'heads'}, dimensions={1}, use_global_device_ids=true | all-gather | bytes 884736 | tf_op jit(solution)/shard_map/all_gather | solution.py:50
  66.6 1.2 copy.21
  67.7 0.1 copy.24
  67.9 35.9 %all-gather.4.cloned.1.call-done = bf16[4,1,1536,512]{3,2,1,0:T(8,128)(2,1)} async-done(((bf16[4,1,192,512]{3,2,1,0:T(8,128)(2,1)}), bf16[4,1,1536,512]{3,2,1,0:T(8,128)(2,1)}) %all-gather.4.cloned.1.call-update) | async-done | bytes 6291472 | tf_op jit(solution)/shard_map/all_gather | solution.py:49
  103.7 4.6 %fusion.5 = f32[6144,256]{0,1:S(1)} fusion(bf16[6144,512]{1,0:T(8,128)(2,1)} %bitcast.25, bf16[512,256]{0,1:T(8,128)(2,1)S(1)} %bitcast.29), kind=kOutput, calls=%fused_computation.16 | convolution fusion | flops 1610612736 | bytes 12845056
  108.4 0.0 copy-start.1
  108.4 0.4 convert_bitcast_fusion
  108.8 0.0 copy-done
  108.8 2.3 %copy-done.1 = bf16[4,1,1536,512]{3,2,1,0:T(8,128)(2,1)S(1)} copy-done((bf16[4,1,1536,512]{3,2,1,0:T(8,128)(2,1)S(1)}, bf16[4,1,1536,512]{3,2,1,0:T(8,128)(2,1)}, u32[]{:S(2)}) %copy-start.1) | copy-done | bytes 6291480
  111.1 1.8 %fusion = bf16[1,6144,2,128]{3,1,2,0:T(8,128)(2,1)S(1)} fusion(bf16[6144,512,1]{1,0,2:T(8,128)(2,1)S(1)} %bitcast.26, bf16[512,2,128]{2,1,0:T(2,128)(2,1)S(1)} %copy-done), kind=kOutput, calls=%fused_computation.1 | convolution fusion | flops 1612185600 | bytes 9699328 | tf_op jit(solution)/shard_map/btr,rhk->bthk/dot_general | solution.py:24
  112.9 26.8 %copy.23 = bf16[1,6144,2,128]{3,2,1,0:T(2,128)(2,1)} copy(bf16[1,6144,2,128]{3,1,2,0:T(8,128)(2,1)S(1)} %fusion) | data formatting | bytes 6291456
  139.7 0.1 broadcast_in_dim.10
  139.9 2.5 %pad_maximum_fusion = bf16[1,6144,2,192]{1,3,2,0:T(8,128)(2,1)} fusion(bf16[1,6144,2,64]{1,3,2,0:T(8,128)(2,1)S(1)} %broadcast_in_dim.10, bf16[1,6144,2,128]{1,3,2,0:T(8,128)(2,1)S(1)} %convert_bitcast_fusion), kind=kLoop, calls=%fused_computation.2 | loop fusion | flops 9437184 | bytes 9437184 | tf_op jit(solution)/shard_map/concatenate | solution.py:27
  (1 shorter events, 0.0 us)
Async XLA Ops:
  7.2 101.6 %copy-start = (bf16[512,2,128]{2,1,0:T(2,128)(2,1)S(1)}, bf16[512,2,128]{2,1,0:T(2,128)(2,1)}, u32[]{:S(2)}) copy-start(bf16[512,2,128]{2,1,0:T(2,128)(2,1)} %param.9) | copy-start | bytes 786436
  7.2 22.9 %copy-start.2 = (bf16[512,2,128]{2,1,0:T(2,128)(2,1)S(1)}, bf16[512,2,128]{2,1,0:T(2,128)(2,1)}, u32[]{:S(2)}) copy-start(bf16[512,2,128]{2,1,0:T(2,128)(2,1)} %param.8) | copy-start | bytes 786436
  7.2 96.6 %all-gather.4.cloned.1.call-start = ((), (), s32[]{:S(2)}) async-start(), calls=%async_computation.2 | async-start | bytes 7077888 | tf_op jit(solution)/shard_map/all_gather | solution.py:49
  26.7 8.3 %all-to-all-start.1 = ((bf16[4,192,64]{1,2,0:T(8,128)(2,1)}), bf16[4,192,64]{1,2,0:T(8,128)(2,1)S(1)}, u32[]{:S(2)}, u32[]{:S(2)}) async-start(bf16[4,192,64]{1,2,0:T(8,128)(2,1)} %param.6), calls=%async_computation.1 | async-start | bytes 262144 | tf_op jit(solution)/shard_map/all_to_all | solution.py:40
  108.4 2.8 %copy-start.1 = (bf16[4,1,1536,512]{3,2,1,0:T(8,128)(2,1)S(1)}, bf16[4,1,1536,512]{3,2,1,0:T(8,128)(2,1)}, u32[]{:S(2)}) copy-start(bf16[4,1,1536,512]{3,2,1,0:T(8,128)(2,1)} %all-gather.4.cloned.1.call-done) | copy-start | bytes 18874372
Sparse Core Ops, SparseCore 0:
  26.8 76.8 all-gather.3
